TPU v7x, 32 devices: a whole 2x2x4 slice. The times are simulated.
32 devices in a mesh: trial: 4 (over x, core), north: 2 (over y), east: 4 (over z).
Axes of the slice: x: 2, y: 2, z: 4, core: 2. Of those that a mesh axis runs over, the one named last changes fastest.
Arguments:
- pair_state: bfloat16 [192, 48, 128], P(('trial', 'north'), 'east'), parts along dimension 0, may hold values from -6 to 6
- in_gain: float32 [128], replicated, may hold values from 0.25 to 1.75
- left_weight: bfloat16 [512, 128], P('trial'), parts along dimension 0, may hold values from -0.5 to 0.5
- right_weight: bfloat16 [512, 128], P('trial'), parts along dimension 0, may hold values from -0.5 to 0.5
- left_gate: bfloat16 [512, 128], P('trial'), parts along dimension 0, may hold values from -0.5 to 0.5
- right_gate: bfloat16 [512, 128], P('trial'), parts along dimension 0, may hold values from -0.5 to 0.5
- mid_gain: float32 [128], replicated, may hold values from 0.25 to 1.75
- out_weight: bfloat16 [512, 128], P('trial'), parts along dimension 0, may hold values from -0.5 to 0.5
- out_gate: bfloat16 [512, 128], P('trial'), parts along dimension 0, may hold values from -0.5 to 0.5
Outputs:
- triangle_out: bfloat16 [192, 48, 128], P(('trial', 'north'), 'east'), parts along dimension 0
There are 4 independent parts, one for each index of `trial`. A program takes and returns all parts, laid end to end along the dimension named above; an argument that names none is the same for every part. Nothing has to cross between parts.
All inputs are finite; a program needn't handle non-finite values.
Results may differ from a plain program's by a relative error of at most 0.015.
Values may be sent and summed in bfloat16 or wider, within the bound.
A program may use at most 64 MiB of HBM per device.

v0:
```python
import jax
import jax.numpy as jnp
from jax import lax
from jax.sharding import PartitionSpec as P


def norm_channels(values, channel_gain):
    centred = values - jnp.mean(values, axis=-1, keepdims=True)
    return (
        centred
        * lax.rsqrt(jnp.mean(centred * centred, axis=-1, keepdims=True) + 1e-05)
        * channel_gain
    )


def make_factors(pair_in, in_gain, left_weight, right_weight, left_gate, right_gate):
    ready = norm_channels(pair_in.astype(jnp.float32), in_gain).astype(jnp.bfloat16)
    ready = lax.optimization_barrier(ready)
    left = jnp.einsum("ijc,cd->ijd", ready, left_weight, preferred_element_type=jnp.float32)
    left = left * jax.nn.sigmoid(
        jnp.einsum("ijc,cd->ijd", ready, left_gate, preferred_element_type=jnp.float32)
    )
    right = jnp.einsum("ijc,cd->ijd", ready, right_weight, preferred_element_type=jnp.float32)
    right = right * jax.nn.sigmoid(
        jnp.einsum("ijc,cd->ijd", ready, right_gate, preferred_element_type=jnp.float32)
    )
    return (ready, left.astype(jnp.bfloat16), right.astype(jnp.bfloat16))


def to_pair(mixed, ready, mid_gain, out_weight, out_gate):
    scaled = norm_channels(mixed.astype(jnp.float32), mid_gain).astype(jnp.bfloat16)
    scaled = lax.optimization_barrier(scaled)
    gate = jax.nn.sigmoid(
        jnp.einsum("ijc,cd->ijd", ready, out_gate, preferred_element_type=jnp.float32)
    )
    return (
        jnp.einsum("ijd,dc->ijc", scaled, out_weight, preferred_element_type=jnp.float32) * gate
    ).astype(jnp.bfloat16)


def local(
    pair_state,
    in_gain,
    left_weight,
    right_weight,
    left_gate,
    right_gate,
    mid_gain,
    out_weight,
    out_gate,
):
    ready, left, right = make_factors(
        pair_state, in_gain, left_weight, right_weight, left_gate, right_gate
    )
    count = pair_state.shape[1] * lax.axis_size("east")
    left_lines, right_lines = (
        lax.all_to_all(left, "east", split_axis=2, concat_axis=1, tiled=True),
        lax.all_to_all(right, "east", split_axis=2, concat_axis=1, tiled=True),
    )
    strip = jnp.einsum(
        "ikd,jkd->ijd",
        left_lines,
        lax.all_gather(right_lines, "north", axis=0, tiled=True),
        preferred_element_type=jnp.float32,
    )
    strip = (strip * count ** (-0.5)).astype(jnp.bfloat16)
    mixed = lax.all_to_all(strip, "east", split_axis=1, concat_axis=2, tiled=True)
    return to_pair(mixed, ready, mid_gain, out_weight, out_gate)


def solution(mesh):
    return jax.shard_map(
        local,
        mesh=mesh,
        in_specs=(
            P(("trial", "north"), "east", None),
            P(),
            P("trial", None),
            P("trial", None),
            P("trial", None),
            P("trial", None),
            P(),
            P("trial", None),
            P("trial", None),
        ),
        out_specs=P(("trial", "north"), "east", None),
        check_vma=False,
    )
```

profile of v0, /device:TPU:0, one launch (start us, length us, event | category | flops | bytes accessed | tf_op | source)
XLA Modules:
  0.0 44.6 jit_solution(821063206014544712)
XLA Ops:
  0.0 1.1 %convert_reduce_fusion = f32[24,12]{0,1:T(8,128)S(1)} fusion(bf16[24,12,128]{2,0,1:T(8,128)(2,1)} %param.9), kind=kLoop, calls=%fused_computation.25 | loop fusion | flops 73440 | bytes 74880 | tf_op jit(solution)/shard_map/reduce_sum | solution.py:8
  1.3 0.6 %copy-done.4 = f32[128]{0:T(128)S(1)} copy-done((f32[128]{0:T(128)S(1)}, f32[128]{0:T(128)}, u32[]{:S(2)}) %copy-start.4) | copy-done | bytes 536
  2.3 0.6 %copy-done.6 = bf16[128,128]{1,0:T(8,128)(2,1)S(1)} copy-done((bf16[128,128]{1,0:T(8,128)(2,1)S(1)}, bf16[128,128]{1,0:T(8,128)(2,1)}, u32[]{:S(2)}) %copy-start.6) | copy-done | bytes 32792
  3.1 0.4 copy.34
  3.5 1.1 %reshape.41 = bf16[4,2,4608]{2,1,0:T(2,128)(2,1)} reshape(bf16[128,12,24]{2,1,0:T(8,128)(2,1)S(1)} %bitcast.55) | data formatting | bytes 147456
  4.7 6.5 %all-to-all-start = ((bf16[4,2,4608]{2,1,0:T(2,128)(2,1)}), bf16[4,2,4608]{2,1,0:T(2,128)(2,1)S(1)}, u32[]{:S(2)}, u32[]{:S(2)}) async-start(bf16[4,2,4608]{2,1,0:T(2,128)(2,1)} %reshape.41), calls=%async_computation | async-start | bytes 147456 | tf_op jit(solution)/shard_map/all_to_all | solution.py:58
  11.3 0.6 %copy-done.7 = bf16[128,128]{1,0:T(8,128)(2,1)S(1)} copy-done((bf16[128,128]{1,0:T(8,128)(2,1)S(1)}, bf16[128,128]{1,0:T(8,128)(2,1)}, u32[]{:S(2)}) %copy-start.7) | copy-done | bytes 32792
  12.1 0.4 copy.37
  12.5 1.1 %reshape.43 = bf16[4,2,4608]{2,1,0:T(2,128)(2,1)} reshape(bf16[128,12,24]{2,1,0:T(8,128)(2,1)S(1)} %bitcast.56) | data formatting | bytes 147456
  13.7 3.2 %all-to-all-done = bf16[4,2,4608]{2,1,0:T(2,128)(2,1)S(1)} async-done(((bf16[4,2,4608]{2,1,0:T(2,128)(2,1)}), bf16[4,2,4608]{2,1,0:T(2,128)(2,1)S(1)}, u32[]{:S(2)}, u32[]{:S(2)}) %all-to-all-start) | async-done | bytes 73760 | tf_op jit(solution)/shard_map/all_to_all | solution.py:58
  16.9 3.3 %all-to-all-start.1 = ((bf16[4,2,4608]{2,1,0:T(2,128)(2,1)}), bf16[4,2,4608]{2,1,0:T(2,128)(2,1)S(1)}, u32[]{:S(2)}, u32[]{:S(2)}) async-start(bf16[4,2,4608]{2,1,0:T(2,128)(2,1)} %reshape.43), calls=%async_computation.1 | async-start | bytes 147456 | tf_op jit(solution)/shard_map/all_to_all | solution.py:57
  20.2 0.6 %reshape.42 = bf16[128,12,24]{2,1,0:T(8,128)(2,1)S(1)} reshape(bf16[4,2,4608]{2,1,0:T(2,128)(2,1)S(1)} %all-to-all-done) | data formatting | bytes 147456
  20.8 0.4 copy.35
  21.5 6.3 %all_gather.3 = bf16[48,48,32]{1,0,2:T(8,128)(2,1)S(1)} all-gather(bf16[24,48,32]{1,0,2:T(8,128)(2,1)S(1)} %copy.36), channel_id=1, replica_groups=mesh['trial'=4,'north'=2,'east'=4] {'north'}, dimensions={0}, use_global_device_ids=true | all-gather | bytes 221184 | tf_op jit(solution)/shard_map/all_gather | solution.py:63
  27.8 0.6 %reshape.44 = bf16[128,12,24]{2,1,0:T(8,128)(2,1)S(1)} reshape(bf16[4,2,4608]{2,1,0:T(2,128)(2,1)S(1)} %all-to-all-done.1) | data formatting | bytes 147456
  28.4 0.4 copy.38
  29.1 0.3 fusion.1
  29.9 10.6 %all_to_all.45 = bf16[4,2,4608]{2,1,0:T(2,128)(2,1)S(1)} all-to-all(bf16[4,2,4608]{2,1,0:T(2,128)(2,1)S(1)} %reshape.45), channel_id=1, replica_groups=mesh['trial'=4,'north'=2,'east'=4] {'east'}, dimensions={0} | all-to-all | bytes 147456 | tf_op jit(solution)/shard_map/all_to_all | solution.py:67
  41.2 0.4 copy.41
  41.6 0.3 reshape.32
  41.9 0.4 copy-done.5
  42.4 0.6 %copy-done.3 = bf16[128,128]{1,0:T(8,128)(2,1)S(1)} copy-done((bf16[128,128]{1,0:T(8,128)(2,1)S(1)}, bf16[128,128]{1,0:T(8,128)(2,1)}, u32[]{:S(2)}) %copy-start.3) | copy-done | bytes 32792
  43.2 0.6 %copy-done.8 = bf16[128,128]{1,0:T(8,128)(2,1)S(1)} copy-done((bf16[128,128]{1,0:T(8,128)(2,1)S(1)}, bf16[128,128]{1,0:T(8,128)(2,1)}, u32[]{:S(2)}) %copy-start.8) | copy-done | bytes 32792
  43.7 0.8 %fusion.14 = bf16[24,12,128]{2,0,1:T(8,128)(2,1)} fusion(f32[24,12,128]{2,0,1:T(8,128)S(1)} %fusion.24, bf16[24,12,128]{2,0,1:T(8,128)(2,1)S(1)} %fusion.22, bf16[128,128]{1,0:T(8,128)(2,1)S(1)} %copy-done.8), kind=kOutput, calls=%fused_computation.18 | convolution fusion | flops 9621504 | bytes 327680 | tf_op jit(solution)/shard_map/ijc,cd->ijd/dot_general | solution.py:34
  (33 shorter events, 3.0 us)
Async XLA Ops:
  0.0 2.1 %copy-start = (bf16[128,128]{1,0:T(8,128)(2,1)S(1)}, bf16[128,128]{1,0:T(8,128)(2,1)}, u32[]{:S(2)}) copy-start(bf16[128,128]{1,0:T(8,128)(2,1)} %param.12) | copy-start | bytes 98308
  0.0 1.1 %copy-start.1 = (bf16[24,12,128]{2,0,1:T(8,128)(2,1)S(1)}, bf16[24,12,128]{2,0,1:T(8,128)(2,1)}, u32[]{:S(2)}) copy-start(bf16[24,12,128]{2,0,1:T(8,128)(2,1)} %param.9) | copy-start | bytes 221188
  1.3 0.7 %copy-start.4 = (f32[128]{0:T(128)S(1)}, f32[128]{0:T(128)}, u32[]{:S(2)}) copy-start(f32[128]{0:T(128)} %param.10) | copy-start | bytes 1540
  2.1 0.8 %copy-start.6 = (bf16[128,128]{1,0:T(8,128)(2,1)S(1)}, bf16[128,128]{1,0:T(8,128)(2,1)}, u32[]{:S(2)}) copy-start(bf16[128,128]{1,0:T(8,128)(2,1)} %param.14) | copy-start | bytes 98308
  4.7 6.5 %copy-start.2 = (bf16[128,128]{1,0:T(8,128)(2,1)S(1)}, bf16[128,128]{1,0:T(8,128)(2,1)}, u32[]{:S(2)}) copy-start(bf16[128,128]{1,0:T(8,128)(2,1)} %param.11) | copy-start | bytes 98308
  4.7 12.2 %all-to-all-start = ((bf16[4,2,4608]{2,1,0:T(2,128)(2,1)}), bf16[4,2,4608]{2,1,0:T(2,128)(2,1)S(1)}, u32[]{:S(2)}, u32[]{:S(2)}) async-start(bf16[4,2,4608]{2,1,0:T(2,128)(2,1)} %reshape.41), calls=%async_computation | async-start | bytes 147456 | tf_op jit(solution)/shard_map/all_to_all | solution.py:58
  11.1 0.8 %copy-start.7 = (bf16[128,128]{1,0:T(8,128)(2,1)S(1)}, bf16[128,128]{1,0:T(8,128)(2,1)}, u32[]{:S(2)}) copy-start(bf16[128,128]{1,0:T(8,128)(2,1)} %param.13) | copy-start | bytes 98308
  16.9 10.9 %all-to-all-start.1 = ((bf16[4,2,4608]{2,1,0:T(2,128)(2,1)}), bf16[4,2,4608]{2,1,0:T(2,128)(2,1)S(1)}, u32[]{:S(2)}, u32[]{:S(2)}) async-start(bf16[4,2,4608]{2,1,0:T(2,128)(2,1)} %reshape.43), calls=%async_computation.1 | async-start | bytes 147456 | tf_op jit(solution)/shard_map/all_to_all | solution.py:57
  41.6 0.7 %copy-start.5 = (f32[128]{0:T(128)S(1)}, f32[128]{0:T(128)}, u32[]{:S(2)}) copy-start(f32[128]{0:T(128)} %param.15) | copy-start | bytes 1540
  42.2 0.8 %copy-start.3 = (bf16[128,128]{1,0:T(8,128)(2,1)S(1)}, bf16[128,128]{1,0:T(8,128)(2,1)}, u32[]{:S(2)}) copy-start(bf16[128,128]{1,0:T(8,128)(2,1)} %param.16) | copy-start | bytes 98308
  43.0 0.8 %copy-start.8 = (bf16[128,128]{1,0:T(8,128)(2,1)S(1)}, bf16[128,128]{1,0:T(8,128)(2,1)}, u32[]{:S(2)}) copy-start(bf16[128,128]{1,0:T(8,128)(2,1)} %param.17) | copy-start | bytes 98308
where the time goes:
time: 45.3 us; the launch traced here: 44.6 us
  blocking collectives  17 us (38%)
  local copies, waits for them, and re-layouts  10.4 us (23%)
  starting transfers between devices  9.77 us (22%)
  waiting for transfers between devices  3.24 us (7%)
  matrix products  2.02 us (4%)
  other arithmetic  1.96 us (4%)
    all_to_all x1, blocking collectives, local(): lax.all_to_all(strip, 'east', split_axis=1, concat_axis=2, tiled=True)  10.6 us
    unnamed x24, local copies, waits for them, and re-layouts  7.31 us
    all_to_all x1, starting transfers between devices, local(): lax.all_to_all(right, 'east', split_axis=2, concat_axis=1, tiled=True)  6.48 us
    all_gather x1, blocking collectives, local(): lax.all_gather(right_lines, 'north', axis=0, tiled=True)  6.34 us
    all_to_all x1, starting transfers between devices, local(): lax.all_to_all(left, 'east', split_axis=2, concat_axis=1, tiled=True)  3.29 us
    all_to_all x1, waiting for transfers between devices, local(): lax.all_to_all(right, 'east', split_axis=2, concat_axis=1, tiled=True)  3.23 us
    reduce_sum x2, other arithmetic, norm_channels(): centred = values - jnp.mean(values, axis=-1, keepdims=True)  1.19 us
  transfers between devices with their start and end apart: 2, of which 1 were waited for; matrix products, arithmetic and copies ran while one was open for 7% of the time, Pallas kernels for 0%

commit v1 on v0

--- a/solution.py
+++ b/solution.py
@@ -64,7 +64,10 @@
         preferred_element_type=jnp.float32,
     )
     strip = (strip * count ** (-0.5)).astype(jnp.bfloat16)
-    mixed = lax.all_to_all(strip, "east", split_axis=1, concat_axis=2, tiled=True)
+    mixed = jnp.concatenate(
+        lax.all_to_all(jnp.stack(jnp.split(strip, lax.axis_size("east"), axis=1)), "east", 0, 0),
+        axis=2,
+    )
     return to_pair(mixed, ready, mid_gain, out_weight, out_gate)
 
 

time: 45.3 us -> 46.4 us (1.024)
  local copies, waits for them, and re-layouts: 10.4 us -> 11.4 us
    another operation x0 -> x5, local copies, waits for them, and re-layouts: none -> 1.27 us  [local(): jnp.stack(jnp.split(strip, lax.axis_size('east'), axis=1))]
where the time goes in v1:
time: 46.4 us; the launch traced here: 45.7 us
  blocking collectives  17 us (37%)
  local copies, waits for them, and re-layouts  11.4 us (25%)
  starting transfers between devices  9.77 us (21%)
  waiting for transfers between devices  3.24 us (7%)
  other arithmetic  2.04 us (4%)
  matrix products  2.02 us (4%)
    all_to_all x1, blocking collectives, local(): lax.all_to_all(jnp.stack(jnp.split(strip, lax.axis_size('east'), axis=1))...  10.6 us
    unnamed x24, local copies, waits for them, and re-layouts  7.32 us
    all_to_all x1, starting transfers between devices, local(): lax.all_to_all(right, 'east', split_axis=2, concat_axis=1, tiled=True)  6.48 us
    all_gather x1, blocking collectives, local(): lax.all_gather(right_lines, 'north', axis=0, tiled=True)  6.34 us
    all_to_all x1, starting transfers between devices, local(): lax.all_to_all(left, 'east', split_axis=2, concat_axis=1, tiled=True)  3.29 us
    all_to_all x1, waiting for transfers between devices, local(): lax.all_to_all(right, 'east', split_axis=2, concat_axis=1, tiled=True)  3.23 us
    another operation x5, local copies, waits for them, and re-layouts, local(): jnp.stack(jnp.split(strip, lax.axis_size('east'), axis=1))  1.27 us
    reduce_sum x2, other arithmetic, norm_channels(): centred = values - jnp.mean(values, axis=-1, keepdims=True)  1.19 us
  transfers between devices with their start and end apart: 2, of which 1 were waited for; matrix products, arithmetic and copies ran while one was open for 7% of the time, Pallas kernels for 0%

profile of v1, /device:TPU:0, one launch (start us, length us, event | category | flops | bytes accessed | tf_op | source)
XLA Modules:
  0.0 45.7 jit_solution(8479987753498319219)
XLA Ops:
  0.0 1.1 %convert_reduce_fusion = f32[24,12]{0,1:T(8,128)S(1)} fusion(bf16[24,12,128]{2,0,1:T(8,128)(2,1)} %param.9), kind=kLoop, calls=%fused_computation.30 | loop fusion | flops 73440 | bytes 74880 | tf_op jit(solution)/shard_map/reduce_sum | solution.py:8
  1.3 0.6 %copy-done.4 = f32[128]{0:T(128)S(1)} copy-done((f32[128]{0:T(128)S(1)}, f32[128]{0:T(128)}, u32[]{:S(2)}) %copy-start.4) | copy-done | bytes 536
  2.3 0.6 %copy-done.6 = bf16[128,128]{1,0:T(8,128)(2,1)S(1)} copy-done((bf16[128,128]{1,0:T(8,128)(2,1)S(1)}, bf16[128,128]{1,0:T(8,128)(2,1)}, u32[]{:S(2)}) %copy-start.6) | copy-done | bytes 32792
  3.1 0.4 copy.36
  3.5 1.1 %reshape.37 = bf16[4,2,4608]{2,1,0:T(2,128)(2,1)} reshape(bf16[128,12,24]{2,1,0:T(8,128)(2,1)S(1)} %bitcast.62) | data formatting | bytes 147456
  4.7 6.5 %all-to-all-start = ((bf16[4,2,4608]{2,1,0:T(2,128)(2,1)}), bf16[4,2,4608]{2,1,0:T(2,128)(2,1)S(1)}, u32[]{:S(2)}, u32[]{:S(2)}) async-start(bf16[4,2,4608]{2,1,0:T(2,128)(2,1)} %reshape.37), calls=%async_computation | async-start | bytes 147456 | tf_op jit(solution)/shard_map/all_to_all | solution.py:58
  11.3 0.6 %copy-done.7 = bf16[128,128]{1,0:T(8,128)(2,1)S(1)} copy-done((bf16[128,128]{1,0:T(8,128)(2,1)S(1)}, bf16[128,128]{1,0:T(8,128)(2,1)}, u32[]{:S(2)}) %copy-start.7) | copy-done | bytes 32792
  12.1 0.4 copy.39
  12.5 1.1 %reshape.39 = bf16[4,2,4608]{2,1,0:T(2,128)(2,1)} reshape(bf16[128,12,24]{2,1,0:T(8,128)(2,1)S(1)} %bitcast.63) | data formatting | bytes 147456
  13.7 3.2 %all-to-all-done = bf16[4,2,4608]{2,1,0:T(2,128)(2,1)S(1)} async-done(((bf16[4,2,4608]{2,1,0:T(2,128)(2,1)}), bf16[4,2,4608]{2,1,0:T(2,128)(2,1)S(1)}, u32[]{:S(2)}, u32[]{:S(2)}) %all-to-all-start) | async-done | bytes 73760 | tf_op jit(solution)/shard_map/all_to_all | solution.py:58
  16.9 3.3 %all-to-all-start.1 = ((bf16[4,2,4608]{2,1,0:T(2,128)(2,1)}), bf16[4,2,4608]{2,1,0:T(2,128)(2,1)S(1)}, u32[]{:S(2)}, u32[]{:S(2)}) async-start(bf16[4,2,4608]{2,1,0:T(2,128)(2,1)} %reshape.39), calls=%async_computation.1 | async-start | bytes 147456 | tf_op jit(solution)/shard_map/all_to_all | solution.py:57
  20.2 0.6 %reshape.38 = bf16[128,12,24]{2,1,0:T(8,128)(2,1)S(1)} reshape(bf16[4,2,4608]{2,1,0:T(2,128)(2,1)S(1)} %all-to-all-done) | data formatting | bytes 147456
  20.8 0.4 copy.37
  21.5 6.3 %all_gather.3 = bf16[48,48,32]{1,0,2:T(8,128)(2,1)S(1)} all-gather(bf16[24,48,32]{1,0,2:T(8,128)(2,1)S(1)} %copy.38), channel_id=1, replica_groups=mesh['trial'=4,'north'=2,'east'=4] {'north'}, dimensions={0}, use_global_device_ids=true | all-gather | bytes 221184 | tf_op jit(solution)/shard_map/all_gather | solution.py:63
  27.8 0.6 %reshape.40 = bf16[128,12,24]{2,1,0:T(8,128)(2,1)S(1)} reshape(bf16[4,2,4608]{2,1,0:T(2,128)(2,1)S(1)} %all-to-all-done.1) | data formatting | bytes 147456
  28.4 0.4 copy.40
  29.1 0.3 fusion.1
  31.0 10.6 %all_to_all.41 = bf16[4,2,4608]{2,1,0:T(2,128)(2,1)S(1)} all-to-all(bf16[4,2,4608]{2,1,0:T(2,128)(2,1)S(1)} %reshape.41), channel_id=1, replica_groups=mesh['trial'=4,'north'=2,'east'=4] {'east'}, dimensions={0} | all-to-all | bytes 147456 | tf_op jit(solution)/shard_map/all_to_all | solution.py:68
  42.3 0.4 copy.46
  42.7 0.3 reshape.30
  43.0 0.4 copy-done.5
  43.5 0.6 %copy-done.3 = bf16[128,128]{1,0:T(8,128)(2,1)S(1)} copy-done((bf16[128,128]{1,0:T(8,128)(2,1)S(1)}, bf16[128,128]{1,0:T(8,128)(2,1)}, u32[]{:S(2)}) %copy-start.3) | copy-done | bytes 32792
  44.3 0.6 %copy-done.8 = bf16[128,128]{1,0:T(8,128)(2,1)S(1)} copy-done((bf16[128,128]{1,0:T(8,128)(2,1)S(1)}, bf16[128,128]{1,0:T(8,128)(2,1)}, u32[]{:S(2)}) %copy-start.8) | copy-done | bytes 32792
  44.9 0.8 %fusion.14 = bf16[24,12,128]{2,0,1:T(8,128)(2,1)} fusion(f32[24,12,128]{2,0,1:T(8,128)S(1)} %fusion.24, bf16[24,12,128]{2,0,1:T(8,128)(2,1)S(1)} %fusion.22, bf16[128,128]{1,0:T(8,128)(2,1)S(1)} %copy-done.8), kind=kOutput, calls=%fused_computation.18 | convolution fusion | flops 9621504 | bytes 327680 | tf_op jit(solution)/shard_map/ijc,cd->ijd/dot_general | solution.py:34
  (38 shorter events, 4.1 us)
Async XLA Ops:
  0.0 2.1 %copy-start = (bf16[128,128]{1,0:T(8,128)(2,1)S(1)}, bf16[128,128]{1,0:T(8,128)(2,1)}, u32[]{:S(2)}) copy-start(bf16[128,128]{1,0:T(8,128)(2,1)} %param.12) | copy-start | bytes 98308
  0.0 1.1 %copy-start.1 = (bf16[24,12,128]{2,0,1:T(8,128)(2,1)S(1)}, bf16[24,12,128]{2,0,1:T(8,128)(2,1)}, u32[]{:S(2)}) copy-start(bf16[24,12,128]{2,0,1:T(8,128)(2,1)} %param.9) | copy-start | bytes 221188
  1.3 0.7 %copy-start.4 = (f32[128]{0:T(128)S(1)}, f32[128]{0:T(128)}, u32[]{:S(2)}) copy-start(f32[128]{0:T(128)} %param.10) | copy-start | bytes 1540
  2.1 0.8 %copy-start.6 = (bf16[128,128]{1,0:T(8,128)(2,1)S(1)}, bf16[128,128]{1,0:T(8,128)(2,1)}, u32[]{:S(2)}) copy-start(bf16[128,128]{1,0:T(8,128)(2,1)} %param.14) | copy-start | bytes 98308
  4.7 6.5 %copy-start.2 = (bf16[128,128]{1,0:T(8,128)(2,1)S(1)}, bf16[128,128]{1,0:T(8,128)(2,1)}, u32[]{:S(2)}) copy-start(bf16[128,128]{1,0:T(8,128)(2,1)} %param.11) | copy-start | bytes 98308
  4.7 12.2 %all-to-all-start = ((bf16[4,2,4608]{2,1,0:T(2,128)(2,1)}), bf16[4,2,4608]{2,1,0:T(2,128)(2,1)S(1)}, u32[]{:S(2)}, u32[]{:S(2)}) async-start(bf16[4,2,4608]{2,1,0:T(2,128)(2,1)} %reshape.37), calls=%async_computation | async-start | bytes 147456 | tf_op jit(solution)/shard_map/all_to_all | solution.py:58
  11.1 0.8 %copy-start.7 = (bf16[128,128]{1,0:T(8,128)(2,1)S(1)}, bf16[128,128]{1,0:T(8,128)(2,1)}, u32[]{:S(2)}) copy-start(bf16[128,128]{1,0:T(8,128)(2,1)} %param.13) | copy-start | bytes 98308
  16.9 10.9 %all-to-all-start.1 = ((bf16[4,2,4608]{2,1,0:T(2,128)(2,1)}), bf16[4,2,4608]{2,1,0:T(2,128)(2,1)S(1)}, u32[]{:S(2)}, u32[]{:S(2)}) async-start(bf16[4,2,4608]{2,1,0:T(2,128)(2,1)} %reshape.39), calls=%async_computation.1 | async-start | bytes 147456 | tf_op jit(solution)/shard_map/all_to_all | solution.py:57
  42.7 0.7 %copy-start.5 = (f32[128]{0:T(128)S(1)}, f32[128]{0:T(128)}, u32[]{:S(2)}) copy-start(f32[128]{0:T(128)} %param.15) | copy-start | bytes 1540
  43.4 0.8 %copy-start.3 = (bf16[128,128]{1,0:T(8,128)(2,1)S(1)}, bf16[128,128]{1,0:T(8,128)(2,1)}, u32[]{:S(2)}) copy-start(bf16[128,128]{1,0:T(8,128)(2,1)} %param.16) | copy-start | bytes 98308
  44.1 0.8 %copy-start.8 = (bf16[128,128]{1,0:T(8,128)(2,1)S(1)}, bf16[128,128]{1,0:T(8,128)(2,1)}, u32[]{:S(2)}) copy-start(bf16[128,128]{1,0:T(8,128)(2,1)} %param.17) | copy-start | bytes 98308
